TPU v7x, 8 devices: a whole 2x2x1 slice. The times are simulated.
8 devices in a mesh: col: 2 (over z, y), row: 2 (over x), depth: 2 (over core).
Axes of the slice: x: 2, y: 2, z: 1, core: 2. Of those that a mesh axis runs over, the one named last changes fastest.
Arguments:
- a_mat: bfloat16 [3072, 6144], P(('depth', 'row', 'col'))
- b_mat: bfloat16 [6144, 5120], P(('depth', 'row', 'col'))
Outputs:
- output: bfloat16 [3072, 5120], P(('depth', 'row', 'col'))
All inputs are finite; a program needn't handle non-finite values.
Results may differ from a plain program's by a relative error of at most 0.001.
Values are sent between devices in bfloat16 or wider.
A program may use at most 1 GiB of HBM per device.

v0:
```python
import jax
import jax.numpy as jnp
from jax import lax
from jax.sharding import PartitionSpec as P


def solution(mesh):
    all_axes = ("depth", "row", "col")
    depth_size = mesh.shape["depth"]
    col_size = mesh.shape["col"]

    def device_block(a_rows, b_rows):
        a_part = lax.all_to_all(a_rows, "depth", 1, 0, tiled=True)
        a_block = lax.all_gather(a_part, "col", axis=0, tiled=True)
        b_part = lax.all_to_all(b_rows, "col", 1, 0, tiled=True)
        b_block = lax.all_gather(b_part, "row", axis=0, tiled=True)
        part_sum = jnp.dot(a_block, b_block, preferred_element_type=jnp.float32)
        rows_dev = a_rows.shape[0]
        n_cols = part_sum.shape[1]
        grouped = part_sum.reshape(col_size, depth_size * rows_dev, n_cols)
        summed = lax.psum_scatter(grouped, "depth", scatter_dimension=1, tiled=True)
        rounded = summed.astype(jnp.bfloat16).reshape(col_size * rows_dev, n_cols)
        return lax.all_to_all(rounded, "col", 0, 1, tiled=True)

    return jax.shard_map(device_block, mesh=mesh, in_specs=(P(all_axes, None), P(all_axes, None)), out_specs=P(all_axes, None), check_vma=False)
```

profile of v0, /device:TPU:1, one launch (start us, length us, event | category | flops | bytes accessed | tf_op | source)
XLA Modules:
  0.0 532.3 jit_solution(16257587519095986258)
XLA Ops:
  6.5 0.0 all-gather.3.cloned.1.call-start
  6.5 6.7 %copy.5 = bf16[384,6144]{0,1:T(8,128)(2,1)} copy(bf16[384,6144]{1,0:T(8,128)(2,1)} %param.2) | data formatting | bytes 9437184 | tf_op args[0]
  13.2 12.1 %all_to_all.54 = bf16[384,2,3072]{0,2,1:T(8,128)(2,1)} all-to-all(bf16[384,2,3072]{0,2,1:T(8,128)(2,1)} %bitcast.17), channel_id=1, replica_groups=mesh['col'=2,'row'=2,'depth'=2] {'depth'}, dimensions={1} | all-to-all | bytes 9437184 | tf_op jit(solution)/shard_map/all_to_all | solution.py:13
  25.3 6.6 %copy.6 = bf16[2,384,3072]{2,1,0:T(8,128)(2,1)} copy(bf16[2,384,3072]{1,2,0:T(8,128)(2,1)} %bitcast.16) | data formatting | bytes 9437184 | tf_op jit(solution)/shard_map/all_to_all | solution.py:13
  31.9 0.0 all-gather.3.cloned.1.call-update
  32.0 0.0 all-gather.5.cloned.1.call-start
  32.0 10.6 %copy.7 = bf16[768,5120]{0,1:T(8,128)(2,1)} copy(bf16[768,5120]{1,0:T(8,128)(2,1)} %param.3) | data formatting | bytes 15728640 | tf_op args[1]
  42.7 183.1 %all_to_all.55 = bf16[768,2,2560]{0,2,1:T(8,128)(2,1)} all-to-all(bf16[768,2,2560]{0,2,1:T(8,128)(2,1)} %bitcast.14), channel_id=1, replica_groups=mesh['col'=2,'row'=2,'depth'=2] {'col'}, dimensions={1} | all-to-all | bytes 15728640 | tf_op jit(solution)/shard_map/all_to_all | solution.py:15
  225.8 10.6 %copy.8 = bf16[2,768,2560]{2,1,0:T(8,128)(2,1)} copy(bf16[2,768,2560]{1,2,0:T(8,128)(2,1)} %bitcast.13) | data formatting | bytes 15728640 | tf_op jit(solution)/shard_map/all_to_all | solution.py:15
  236.4 0.0 all-gather.5.cloned.1.call-update
  236.4 0.0 reduce-scatter.2.cloned.1.call-start
  236.5 0.0 all-gather.3.cloned.1.call-done
  236.5 185.4 %all-gather.5.cloned.1.call-done = bf16[3072,2560]{1,0:T(8,128)(2,1)} async-done(((bf16[1536,2560]{1,0:T(8,128)(2,1)}), bf16[3072,2560]{1,0:T(8,128)(2,1)}) %all-gather.5.cloned.1.call-update) | async-done | bytes 15728656 | tf_op jit(solution)/shard_map/all_gather | solution.py:16
  421.9 31.9 %fusion = f32[1536,2560]{1,0:T(8,128)} fusion(bf16[1536,3072]{1,0:T(8,128)(2,1)} %all-gather.3.cloned.1.call-done, bf16[3072,2560]{1,0:T(8,128)(2,1)} %all-gather.5.cloned.1.call-done), kind=kOutput, calls=%fused_computation | convolution fusion | flops 24159191040 | bytes 40894464 | tf_op jit(solution)/shard_map/dot_general | solution.py:17
  453.8 0.0 reduce-scatter.2.cloned.1.call-update
  453.9 18.5 %reduce-scatter.2.cloned.1.call-done = f32[2,384,2560]{2,1,0:T(8,128)} async-done(((f32[2,768,2560]{2,1,0:T(8,128)}), f32[2,384,2560]{2,1,0:T(8,128)}) %reduce-scatter.2.cloned.1.call-update) | async-done | bytes 7864336 | tf_op jit(solution)/shard_map/reduce_scatter | solution.py:21
  472.4 3.7 convert_element_type.3
  476.1 47.2 %all_to_all.56 = bf16[2,384,2560]{2,1,0:T(8,128)(2,1)S(1)} all-to-all(bf16[2,384,2560]{2,1,0:T(8,128)(2,1)S(1)} %convert_element_type.3), channel_id=1, replica_groups=mesh['col'=2,'row'=2,'depth'=2] {'col'}, dimensions={0} | all-to-all | bytes 7864320 | tf_op jit(solution)/shard_map/all_to_all | solution.py:23
  523.3 2.5 copy.10
Async XLA Ops:
  6.5 230.0 %all-gather.3.cloned.1.call-start = ((), (), s32[]{:S(2)}) async-start(), calls=%async_computation.4 | async-start | bytes 14155776 | tf_op jit(solution)/shard_map/all_gather | solution.py:14
  32.0 390.0 %all-gather.5.cloned.1.call-start = ((), (), s32[]{:S(2)}) async-start(), calls=%async_computation.5 | async-start | bytes 23592960 | tf_op jit(solution)/shard_map/all_gather | solution.py:16
  236.4 236.0 %reduce-scatter.2.cloned.1.call-start = ((), (), s32[]{:S(2)}) async-start(), calls=%async_computation.6 | async-start | bytes 23592960 | tf_op jit(solution)/shard_map/reduce_scatter | solution.py:21
Sparse Core Ops, SparseCore 0:
  32.1 202.1 all-gather.2
  236.5 185.3 all-gather.4
  454.0 18.3 reduce-scatter.1
where the time goes:
time: 535 us; the launch traced here: 532 us
  blocking collectives  242 us (45%)
  waiting for transfers between devices  204 us (38%)
  local copies, waits for them, and re-layouts  37.1 us (7%)
  matrix products  31.9 us (6%)
  between operations  13.1 us (2%)
    all_gather x1, waiting for transfers between devices, device_block(): b_block = lax.all_gather(b_part, 'row', axis=0, tiled=True)  185 us
    all_to_all x1, blocking collectives, device_block(): b_part = lax.all_to_all(b_rows, 'col', 1, 0, tiled=True)  183 us
    all_to_all x1, blocking collectives, device_block(): return lax.all_to_all(rounded, 'col', 0, 1, tiled=True)  47.2 us
    dot_general x1, matrix products, device_block(): part_sum = jnp.dot(a_block, b_block, preferred_element_type=jnp.float32)  31.9 us
    reduce_scatter x1, waiting for transfers between devices, device_block(): summed = lax.psum_scatter(grouped, 'depth', scatter_dimension=1, tiled=True)  18.5 us
    unnamed x2, local copies, waits for them, and re-layouts  17.4 us
    all_to_all x1, blocking collectives, device_block(): a_part = lax.all_to_all(a_rows, 'depth', 1, 0, tiled=True)  12.1 us
  transfers between devices with their start and end apart: 3, of which 2 were waited for; matrix products, arithmetic and copies ran while one was open for 4% of the time, Pallas kernels for 0%

commit v1 on v0

v1 whole, which is shorter than its diff:
```python
import jax
import jax.numpy as jnp
from jax import lax
from jax.experimental import pallas as pl
from jax.experimental.pallas import tpu as pltpu
from jax.sharding import PartitionSpec as P

MESH = pl.DeviceIdType.MESH
TN = 512
LAG = 2


def kernel(a_ref, b_ref, c_ref, b_buf, a_own, a_nbr, p_own, p_snd, p_rcv, stage,
           ld_a, ld_b, a_snd_sem, a_rcv_sem, x_snd_sem, x_rcv_sem, d_snd_sem, d_rcv_sem,
           r_snd_sem, r_rcv_sem, c_snd_sem, c_rcv_sem, out_sem):
    depth, row, col = lax.axis_index("depth"), lax.axis_index("row"), lax.axis_index("col")
    to_y, to_x, to_d = {"col": 1 - col}, {"row": 1 - row}, {"depth": 1 - depth}
    rows, k_rows = a_ref.shape[0], b_ref.shape[0]
    half = rows // 2
    n_chunks = b_buf.shape[0]

    def k_block(place, c):
        d = 1 - depth if place % 2 else depth
        r = 1 - row if place // 2 else row
        return pl.ds(pl.multiple_of((d * 4 + r * 2 + c) * k_rows, k_rows), k_rows)

    def slot(place):
        return pl.ds(place * k_rows, k_rows)

    def cols(j):
        return pl.ds(pl.multiple_of(j * TN, TN), TN)

    def load_a(place):
        return pltpu.make_async_copy(a_ref.at[:, k_block(place, col)], a_own.at[:, slot(place)], ld_a.at[place])

    def load_b(j):
        return pltpu.make_async_copy(b_ref.at[:, cols(j)], b_buf.at[j, slot(0), :], ld_b.at[j])

    def send_a(h, place):
        return pltpu.make_async_remote_copy(
            src_ref=a_ref.at[pl.ds(h * half, half), k_block(place, 1 - col)],
            dst_ref=a_nbr.at[pl.ds(h * half, half), slot(place)],
            send_sem=a_snd_sem.at[h, place], recv_sem=a_rcv_sem.at[h, place], device_id=to_y, device_id_type=MESH)

    def send_x(j):
        return pltpu.make_async_remote_copy(
            src_ref=b_ref.at[:, cols(j)], dst_ref=b_buf.at[j, slot(2), :],
            send_sem=x_snd_sem.at[j], recv_sem=x_rcv_sem.at[j], device_id=to_x, device_id_type=MESH)

    def send_d(j):
        return pltpu.make_async_remote_copy(
            src_ref=b_ref.at[:, cols(j)], dst_ref=b_buf.at[j, slot(1), :],
            send_sem=d_snd_sem.at[j], recv_sem=d_rcv_sem.at[j], device_id=to_d, device_id_type=MESH)

    def relay(j):
        return pltpu.make_async_remote_copy(
            src_ref=b_buf.at[j, slot(2), :], dst_ref=b_buf.at[j, slot(3), :],
            send_sem=r_snd_sem.at[j], recv_sem=r_rcv_sem.at[j], device_id=to_d, device_id_type=MESH)

    def send_c(j, h):
        return pltpu.make_async_remote_copy(
            src_ref=p_snd.at[j, pl.ds(h * half, half), :], dst_ref=p_rcv.at[j, pl.ds(h * half, half), :],
            send_sem=c_snd_sem.at[j, h], recv_sem=c_rcv_sem.at[j, h], device_id=to_y, device_id_type=MESH)

    def store_c(j, s):
        return pltpu.make_async_copy(stage.at[s], c_ref.at[:, cols(j)], out_sem.at[s])

    for place in range(4):
        load_a(place).start()

    @pl.loop(0, n_chunks)
    def _(j):
        load_b(j).start()

    barrier = pltpu.get_barrier_semaphore()
    for peer in (to_y, to_x, to_d):
        pl.semaphore_signal(barrier, inc=1, device_id=peer, device_id_type=MESH)
    pl.semaphore_wait(barrier, 3)

    for h in range(2):
        for place in range(4):
            send_a(h, place).start()

    @pl.loop(0, n_chunks)
    def _(j):
        send_x(j).start()
        send_d(j).start()

    for place in range(4):
        load_a(place).wait()

    def part(j, h):
        p_snd[j, pl.ds(h * half, half), :] = jnp.dot(
            a_nbr[pl.ds(h * half, half), :], b_buf[j], preferred_element_type=jnp.float32)

    @pl.loop(0, n_chunks)
    def _(j):
        send_x(j).wait_recv()
        relay(j).start()
        load_b(j).wait()
        send_d(j).wait_recv()
        relay(j).wait_recv()

        @pl.when(j == 0)
        def _():
            for place in range(4):
                send_a(0, place).wait_recv()

        @pl.when(j == LAG)
        def _():
            for place in range(4):
                send_a(1, place).wait_recv()

        part(j, 0)

        @pl.when(j >= LAG)
        def _():
            part(j - LAG, 1)

        p_own[j] = jnp.dot(a_own[...], b_buf[j], preferred_element_type=jnp.float32)
        send_c(j, 0).start()

        @pl.when(j >= LAG)
        def _():
            send_c(j - LAG, 1).start()

    @pl.loop(n_chunks - LAG, n_chunks)
    def _(j):
        part(j, 1)

    def finish(j):
        s = lax.rem(j, 2)

        @pl.when(j >= 2)
        def _():
            store_c(j - 2, s).wait()

        for h in range(2):
            send_c(j, h).wait_recv()
            piece = pl.ds(h * half, half)
            stage[s, piece, :] = (p_own[j, piece, :] + p_rcv[j, piece, :]).astype(stage.dtype)
        store_c(j, s).start()

    finish(0)
    for j in range(n_chunks - LAG, n_chunks):
        send_c(j, 1).start()

    @pl.loop(1, n_chunks)
    def _(j):
        finish(j)

    for h in range(2):
        for place in range(4):
            send_a(h, place).wait_send()

    @pl.loop(0, n_chunks)
    def _(j):
        send_x(j).wait_send()
        send_d(j).wait_send()
        relay(j).wait_send()
        for h in range(2):
            send_c(j, h).wait_send()

    for j in range(n_chunks - 2, n_chunks):
        store_c(j, j % 2).wait()


def solution(mesh):
    all_axes = ("depth", "row", "col")

    def device_block(a_rows, b_rows):
        rows, depth = a_rows.shape
        k_rows, n = b_rows.shape
        k = 4 * k_rows
        n_chunks = n // TN
        dma = pltpu.SemaphoreType.DMA
        return pl.pallas_call(
            kernel,
            out_shape=jax.ShapeDtypeStruct((rows, n), jnp.bfloat16),
            in_specs=[pl.BlockSpec(memory_space=pl.ANY)] * 2,
            out_specs=pl.BlockSpec(memory_space=pl.ANY),
            scratch_shapes=[
                pltpu.VMEM((n_chunks, k, TN), jnp.bfloat16),
                pltpu.VMEM((rows, k), jnp.bfloat16),
                pltpu.VMEM((rows, k), jnp.bfloat16),
                pltpu.VMEM((n_chunks, rows, TN), jnp.float32),
                pltpu.VMEM((n_chunks, rows, TN), jnp.float32),
                pltpu.VMEM((n_chunks, rows, TN), jnp.float32),
                pltpu.VMEM((2, rows, TN), jnp.bfloat16),
                dma((4,)), dma((n_chunks,)),
                dma((2, 4)), dma((2, 4)),
                dma((n_chunks,)), dma((n_chunks,)),
                dma((n_chunks,)), dma((n_chunks,)),
                dma((n_chunks,)), dma((n_chunks,)),
                dma((n_chunks, 2)), dma((n_chunks, 2)),
                dma((2,)),
            ],
            compiler_params=pltpu.CompilerParams(
                collective_id=0, has_side_effects=True, vmem_limit_bytes=67043328),
        )(a_rows, b_rows)

    return jax.shard_map(device_block, mesh=mesh, in_specs=(P(all_axes, None), P(all_axes, None)),
                         out_specs=P(all_axes, None), check_vma=False)
```

time: 535 us -> 231 us (0.43)
  blocking collectives: 242 us -> 0 us
  Pallas kernels: 0 us -> 225 us
  waiting for transfers between devices: 204 us -> 0 us
  local copies, waits for them, and re-layouts: 37.1 us -> 4.29 us
  matrix products: 31.9 us -> 0 us
  between operations: 13.1 us -> 0.01 us
    all_to_all x3 -> x0, blocking collectives: 242 us -> none  [the longest x1 183 us: device_block(): b_part = lax.all_to_all(b_rows, 'col', 1, 0, tiled=True)]
    pallas_call x0 -> x1, Pallas kernels: none -> 225 us  [device_block(): pl.pallas_call(kernel, out_shape=jax.ShapeDtypeStruct((rows, n), jnp.bflo...]
    all_gather x2 -> x0, waiting for transfers between devices: 185 us -> none  [the longest x1 185 us: device_block(): b_block = lax.all_gather(b_part, 'row', axis=0, tiled=True)]
    dot_general x1 -> x0, matrix products: 31.9 us -> none  [device_block(): part_sum = jnp.dot(a_block, b_block, preferred_element_type=jnp.float32)]
    all_to_all x3 -> x0, local copies, waits for them, and re-layouts: 19.7 us -> none  [the longest x1 10.6 us: device_block(): b_part = lax.all_to_all(b_rows, 'col', 1, 0, tiled=True)]
    reduce_scatter x1 -> x0, waiting for transfers between devices: 18.5 us -> none  [device_block(): summed = lax.psum_scatter(grouped, 'depth', scatter_dimension=1, tiled=True)]
    unnamed x2 -> x1, local copies, waits for them, and re-layouts: 17.4 us -> 4.29 us
  transfers between devices with their start and end apart: 3 -> 0, of which waited for: 2 -> 0; matrix products, arithmetic and copies ran while one was open for 4% -> 0% of each run, Pallas kernels for 0% -> 0%
where the time goes in v1:
time: 231 us; the launch traced here: 229 us
  Pallas kernels  225 us (97%)
  local copies, waits for them, and re-layouts  4.29 us (2%)
    pallas_call x1, Pallas kernels, device_block(): pl.pallas_call(kernel, out_shape=jax.ShapeDtypeStruct((rows, n), jnp.bflo...  225 us

profile of v1, /device:TPU:1, one launch (start us, length us, event | category | flops | bytes accessed | tf_op | source)
XLA Modules:
  0.0 228.8 jit_solution(12417350637014694482)
XLA Ops:
  0.0 224.5 %shard_map.28 = bf16[384,5120]{1,0:T(8,128)(2,1)} custom-call(bf16[384,6144]{1,0:T(8,128)(2,1)} %a_ref.1, bf16[768,5120]{1,0:T(8,128)(2,1)} %b_ref.1), custom_call_target="tpu_custom_call" | custom-call | tf_op jit(solution)/shard_map/pallas_call | solution.py:177
  224.5 4.3 %copy.4 = bf16[384,5120]{1,0:T(8,128)(2,1)} copy(bf16[384,5120]{1,0:T(8,128)(2,1)} %shard_map.28) | data formatting | bytes 7864320

commit v2 on v1

--- a/solution.py
+++ b/solution.py
@@ -10,9 +10,9 @@
 LAG = 2
 
 
-def kernel(a_ref, b_ref, c_ref, b_buf, a_own, a_nbr, p_own, p_snd, p_rcv, stage,
-           ld_a, ld_b, a_snd_sem, a_rcv_sem, x_snd_sem, x_rcv_sem, d_snd_sem, d_rcv_sem,
-           r_snd_sem, r_rcv_sem, c_snd_sem, c_rcv_sem, out_sem):
+def kernel(a_ref, b_ref, c_ref, b_buf, a_own, a_nbr, p_own, p_snd, p_rcv, a_first,
+           ld_f, ld_a, ld_b, a_snd_sem, a_rcv_sem, x_snd_sem, x_rcv_sem, d_snd_sem, d_rcv_sem,
+           r_snd_sem, r_rcv_sem, c_snd_sem, c_rcv_sem):
     depth, row, col = lax.axis_index("depth"), lax.axis_index("row"), lax.axis_index("col")
     to_y, to_x, to_d = {"col": 1 - col}, {"row": 1 - row}, {"depth": 1 - depth}
     rows, k_rows = a_ref.shape[0], b_ref.shape[0]
@@ -36,9 +36,13 @@
     def load_b(j):
         return pltpu.make_async_copy(b_ref.at[:, cols(j)], b_buf.at[j, slot(0), :], ld_b.at[j])
 
+    def load_first():
+        return pltpu.make_async_copy(a_ref.at[pl.ds(0, half), k_block(0, 1 - col)], a_first, ld_f)
+
     def send_a(h, place):
+        first = h == 0 and place == 0
         return pltpu.make_async_remote_copy(
-            src_ref=a_ref.at[pl.ds(h * half, half), k_block(place, 1 - col)],
+            src_ref=a_first if first else a_ref.at[pl.ds(h * half, half), k_block(place, 1 - col)],
             dst_ref=a_nbr.at[pl.ds(h * half, half), slot(place)],
             send_sem=a_snd_sem.at[h, place], recv_sem=a_rcv_sem.at[h, place], device_id=to_y, device_id_type=MESH)
 
@@ -62,21 +66,14 @@
             src_ref=p_snd.at[j, pl.ds(h * half, half), :], dst_ref=p_rcv.at[j, pl.ds(h * half, half), :],
             send_sem=c_snd_sem.at[j, h], recv_sem=c_rcv_sem.at[j, h], device_id=to_y, device_id_type=MESH)
 
-    def store_c(j, s):
-        return pltpu.make_async_copy(stage.at[s], c_ref.at[:, cols(j)], out_sem.at[s])
-
-    for place in range(4):
-        load_a(place).start()
-
-    @pl.loop(0, n_chunks)
-    def _(j):
-        load_b(j).start()
+    load_first().start()
 
     barrier = pltpu.get_barrier_semaphore()
     for peer in (to_y, to_x, to_d):
         pl.semaphore_signal(barrier, inc=1, device_id=peer, device_id_type=MESH)
     pl.semaphore_wait(barrier, 3)
 
+    load_first().wait()
     for h in range(2):
         for place in range(4):
             send_a(h, place).start()
@@ -84,7 +81,14 @@
     @pl.loop(0, n_chunks)
     def _(j):
         send_x(j).start()
+
+    for place in range(4):
+        load_a(place).start()
+
+    @pl.loop(0, n_chunks)
+    def _(j):
         send_d(j).start()
+        load_b(j).start()
 
     for place in range(4):
         load_a(place).wait()
@@ -129,17 +133,10 @@
         part(j, 1)
 
     def finish(j):
-        s = lax.rem(j, 2)
-
-        @pl.when(j >= 2)
-        def _():
-            store_c(j - 2, s).wait()
-
         for h in range(2):
             send_c(j, h).wait_recv()
             piece = pl.ds(h * half, half)
-            stage[s, piece, :] = (p_own[j, piece, :] + p_rcv[j, piece, :]).astype(stage.dtype)
-        store_c(j, s).start()
+            c_ref[piece, cols(j)] = (p_own[j, piece, :] + p_rcv[j, piece, :]).astype(c_ref.dtype)
 
     finish(0)
     for j in range(n_chunks - LAG, n_chunks):
@@ -161,9 +158,6 @@
         for h in range(2):
             send_c(j, h).wait_send()
 
-    for j in range(n_chunks - 2, n_chunks):
-        store_c(j, j % 2).wait()
-
 
 def solution(mesh):
     all_axes = ("depth", "row", "col")
@@ -176,9 +170,9 @@
         dma = pltpu.SemaphoreType.DMA
         return pl.pallas_call(
             kernel,
-            out_shape=jax.ShapeDtypeStruct((rows, n), jnp.bfloat16),
+            out_shape=pltpu.VMEM((rows, n), jnp.bfloat16),
             in_specs=[pl.BlockSpec(memory_space=pl.ANY)] * 2,
-            out_specs=pl.BlockSpec(memory_space=pl.ANY),
+            out_specs=pl.BlockSpec(memory_space=pltpu.VMEM),
             scratch_shapes=[
                 pltpu.VMEM((n_chunks, k, TN), jnp.bfloat16),
                 pltpu.VMEM((rows, k), jnp.bfloat16),
@@ -186,17 +180,16 @@
                 pltpu.VMEM((n_chunks, rows, TN), jnp.float32),
                 pltpu.VMEM((n_chunks, rows, TN), jnp.float32),
                 pltpu.VMEM((n_chunks, rows, TN), jnp.float32),
-                pltpu.VMEM((2, rows, TN), jnp.bfloat16),
-                dma((4,)), dma((n_chunks,)),
+                pltpu.VMEM((rows // 2, k_rows), jnp.bfloat16),
+                dma, dma((4,)), dma((n_chunks,)),
                 dma((2, 4)), dma((2, 4)),
                 dma((n_chunks,)), dma((n_chunks,)),
                 dma((n_chunks,)), dma((n_chunks,)),
                 dma((n_chunks,)), dma((n_chunks,)),
                 dma((n_chunks, 2)), dma((n_chunks, 2)),
-                dma((2,)),
             ],
             compiler_params=pltpu.CompilerParams(
-                collective_id=0, has_side_effects=True, vmem_limit_bytes=67043328),
+                collective_id=0, has_side_effects=True, vmem_limit_bytes=67043328 - 2 * rows * n),
         )(a_rows, b_rows)
 
     return jax.shard_map(device_block, mesh=mesh, in_specs=(P(all_axes, None), P(all_axes, None)),

time: 231 us -> 228 us (0.987)
  local copies, waits for them, and re-layouts: 4.29 us -> 1.93 us
    unnamed x1, local copies, waits for them, and re-layouts: 4.29 us -> 1.93 us
where the time goes in v2:
time: 228 us; the launch traced here: 226 us
  Pallas kernels  224 us (98%)
    pallas_call x1, Pallas kernels, device_block(): pl.pallas_call(kernel, out_shape=pltpu.VMEM((rows, n), jnp.bfloat16), in_...  224 us

profile of v2, /device:TPU:1, one launch (start us, length us, event | category | flops | bytes accessed | tf_op | source)
XLA Modules:
  0.0 225.7 jit_solution(14884512421593346216)
XLA Ops:
  0.0 223.8 %shard_map.28 = bf16[384,5120]{1,0:T(8,128)(2,1)S(1)} custom-call(bf16[384,6144]{1,0:T(8,128)(2,1)} %a_ref.1, bf16[768,5120]{1,0:T(8,128)(2,1)} %b_ref.1), custom_call_target="tpu_custom_call" | custom-call | tf_op jit(solution)/shard_map/pallas_call | solution.py:171
  223.8 1.9 copy.4

commit v3 on v2

--- a/solution.py
+++ b/solution.py
@@ -8,11 +8,13 @@
 MESH = pl.DeviceIdType.MESH
 TN = 512
 LAG = 2
-
-
-def kernel(a_ref, b_ref, c_ref, b_buf, a_own, a_nbr, p_own, p_snd, p_rcv, a_first,
+EXTRA = 96
+
+
+def kernel(a_ref, b_ref, c_ref, b_buf, a_own, a_nbr, p_own, p_snd, p_rcv, a_first, a_fwd,
            ld_f, ld_a, ld_b, a_snd_sem, a_rcv_sem, x_snd_sem, x_rcv_sem, d_snd_sem, d_rcv_sem,
-           r_snd_sem, r_rcv_sem, c_snd_sem, c_rcv_sem):
+           r_snd_sem, r_rcv_sem, c_snd_sem, c_rcv_sem, f_snd_sem, f_rcv_sem, fwd_sem,
+           pair_sem, core_sem):
     depth, row, col = lax.axis_index("depth"), lax.axis_index("row"), lax.axis_index("col")
     to_y, to_x, to_d = {"col": 1 - col}, {"row": 1 - row}, {"depth": 1 - depth}
     rows, k_rows = a_ref.shape[0], b_ref.shape[0]
@@ -39,12 +41,29 @@
     def load_first():
         return pltpu.make_async_copy(a_ref.at[pl.ds(0, half), k_block(0, 1 - col)], a_first, ld_f)
 
-    def send_a(h, place):
-        first = h == 0 and place == 0
-        return pltpu.make_async_remote_copy(
-            src_ref=a_first if first else a_ref.at[pl.ds(h * half, half), k_block(place, 1 - col)],
-            dst_ref=a_nbr.at[pl.ds(h * half, half), slot(place)],
-            send_sem=a_snd_sem.at[h, place], recv_sem=a_rcv_sem.at[h, place], device_id=to_y, device_id_type=MESH)
+    pieces = [(0, half, p) for p in range(4)] + [(half, half, p) for p in range(3)]
+    pieces += [(half, half - EXTRA, 3), (rows - EXTRA, EXTRA, 3)]
+    last = len(pieces) - 1
+
+    def send_a(i):
+        start, size, place = pieces[i]
+        return pltpu.make_async_remote_copy(
+            src_ref=a_first if i == 0 else a_ref.at[pl.ds(start, size), k_block(place, 1 - col)],
+            dst_ref=a_nbr.at[pl.ds(start, size), slot(place)],
+            send_sem=a_snd_sem.at[i], recv_sem=a_rcv_sem.at[i], device_id=to_y, device_id_type=MESH)
+
+    def hand_over():
+        start, size, place = pieces[last]
+        return pltpu.make_async_remote_copy(
+            src_ref=a_ref.at[pl.ds(start, size), k_block(place, 1 - col)], dst_ref=a_fwd,
+            send_sem=f_snd_sem, recv_sem=f_rcv_sem, device_id=to_d, device_id_type=MESH)
+
+    def send_for_other():
+        start, size, place = pieces[last]
+        return pltpu.make_async_remote_copy(
+            src_ref=a_fwd, dst_ref=a_nbr.at[pl.ds(start, size), slot(place)],
+            send_sem=fwd_sem, recv_sem=a_rcv_sem.at[last],
+            device_id={"col": 1 - col, "depth": 0}, device_id_type=MESH)
 
     def send_x(j):
         return pltpu.make_async_remote_copy(
@@ -69,14 +88,25 @@
     load_first().start()
 
     barrier = pltpu.get_barrier_semaphore()
-    for peer in (to_y, to_x, to_d):
+    for peer in (to_y, {"depth": 0, "row": lax.rem(row + 1 - depth, 2)}):
         pl.semaphore_signal(barrier, inc=1, device_id=peer, device_id_type=MESH)
-    pl.semaphore_wait(barrier, 3)
+    pl.semaphore_wait(barrier, 3 - 2 * depth)
 
     load_first().wait()
-    for h in range(2):
-        for place in range(4):
-            send_a(h, place).start()
+    for i in range(last):
+        send_a(i).start()
+
+    @pl.when(depth == 0)
+    def _():
+        hand_over().start()
+        pl.semaphore_signal(pair_sem, inc=1, device_id=to_x, device_id_type=MESH)
+        pl.semaphore_wait(pair_sem, 1)
+        pl.semaphore_signal(core_sem, inc=1, device_id=to_d, device_id_type=MESH)
+
+    @pl.when(depth == 1)
+    def _():
+        send_a(last).start()
+        pl.semaphore_wait(core_sem, 1)
 
     @pl.loop(0, n_chunks)
     def _(j):
@@ -89,6 +119,11 @@
     def _(j):
         send_d(j).start()
         load_b(j).start()
+
+    @pl.when(depth == 1)
+    def _():
+        hand_over().wait_recv()
+        send_for_other().start()
 
     for place in range(4):
         load_a(place).wait()
@@ -107,13 +142,13 @@
 
         @pl.when(j == 0)
         def _():
-            for place in range(4):
-                send_a(0, place).wait_recv()
+            for i in range(4):
+                send_a(i).wait_recv()
 
         @pl.when(j == LAG)
         def _():
-            for place in range(4):
-                send_a(1, place).wait_recv()
+            for i in range(4, last + 1):
+                send_a(i).wait_recv()
 
         part(j, 0)
 
@@ -146,9 +181,17 @@
     def _(j):
         finish(j)
 
-    for h in range(2):
-        for place in range(4):
-            send_a(h, place).wait_send()
+    for i in range(last):
+        send_a(i).wait_send()
+
+    @pl.when(depth == 0)
+    def _():
+        hand_over().wait_send()
+
+    @pl.when(depth == 1)
+    def _():
+        send_a(last).wait_send()
+        send_for_other().wait_send()
 
     @pl.loop(0, n_chunks)
     def _(j):
@@ -181,12 +224,15 @@
                 pltpu.VMEM((n_chunks, rows, TN), jnp.float32),
                 pltpu.VMEM((n_chunks, rows, TN), jnp.float32),
                 pltpu.VMEM((rows // 2, k_rows), jnp.bfloat16),
+                pltpu.VMEM((EXTRA, k_rows), jnp.bfloat16),
                 dma, dma((4,)), dma((n_chunks,)),
-                dma((2, 4)), dma((2, 4)),
+                dma((9,)), dma((9,)),
                 dma((n_chunks,)), dma((n_chunks,)),
                 dma((n_chunks,)), dma((n_chunks,)),
                 dma((n_chunks,)), dma((n_chunks,)),
                 dma((n_chunks, 2)), dma((n_chunks, 2)),
+                dma, dma, dma,
+                pltpu.SemaphoreType.REGULAR, pltpu.SemaphoreType.REGULAR,
             ],
             compiler_params=pltpu.CompilerParams(
                 collective_id=0, has_side_effects=True, vmem_limit_bytes=67043328 - 2 * rows * n),

time: 228 us -> 226 us (level); the launches traced: 226 us -> 226 us
  no operation moved by 1% of the time
where the time goes in v3:
time: 226 us
  Pallas kernels  224 us (99%)
    pallas_call x1, Pallas kernels, device_block(): pl.pallas_call(kernel, out_shape=pltpu.VMEM((rows, n), jnp.bfloat16), in_...  224 us

profile of v3, /device:TPU:1, one launch (start us, length us, event | category | flops | bytes accessed | tf_op | source)
XLA Modules:
  0.0 226.4 jit_solution(8992061473992554645)
XLA Ops:
  0.0 224.5 %shard_map.28 = bf16[384,5120]{1,0:T(8,128)(2,1)S(1)} custom-call(bf16[384,6144]{1,0:T(8,128)(2,1)} %a_ref.1, bf16[768,5120]{1,0:T(8,128)(2,1)} %b_ref.1), custom_call_target="tpu_custom_call" | custom-call | tf_op jit(solution)/shard_map/pallas_call | solution.py:214
  224.5 1.9 copy.4

commit v4 on v3

--- a/solution.py
+++ b/solution.py
@@ -8,7 +8,7 @@
 MESH = pl.DeviceIdType.MESH
 TN = 512
 LAG = 2
-EXTRA = 96
+EXTRA = 48
 
 
 def kernel(a_ref, b_ref, c_ref, b_buf, a_own, a_nbr, p_own, p_snd, p_rcv, a_first, a_fwd,

time: 226 us -> 227 us (level)
  no operation moved by 1% of the time
where the time goes in v4:
time: 227 us; the launch traced here: 226 us
  Pallas kernels  225 us (99%)
    pallas_call x1, Pallas kernels, device_block(): pl.pallas_call(kernel, out_shape=pltpu.VMEM((rows, n), jnp.bfloat16), in_...  225 us

profile of v4, /device:TPU:1, one launch (start us, length us, event | category | flops | bytes accessed | tf_op | source)
XLA Modules:
  0.0 226.5 jit_solution(18099809860145465267)
XLA Ops:
  0.0 224.6 %shard_map.28 = bf16[384,5120]{1,0:T(8,128)(2,1)S(1)} custom-call(bf16[384,6144]{1,0:T(8,128)(2,1)} %a_ref.1, bf16[768,5120]{1,0:T(8,128)(2,1)} %b_ref.1), custom_call_target="tpu_custom_call" | custom-call | tf_op jit(solution)/shard_map/pallas_call | solution.py:214
  224.6 1.9 copy.4

commit v5 on v3

--- a/solution.py
+++ b/solution.py
@@ -8,6 +8,7 @@
 MESH = pl.DeviceIdType.MESH
 TN = 512
 LAG = 2
+AHEAD = 2
 EXTRA = 96
 
 
@@ -115,10 +116,12 @@
     for place in range(4):
         load_a(place).start()
 
-    @pl.loop(0, n_chunks)
-    def _(j):
+    def bring(j):
         send_d(j).start()
         load_b(j).start()
+
+    for j in range(AHEAD):
+        bring(j)
 
     @pl.when(depth == 1)
     def _():
@@ -136,6 +139,11 @@
     def _(j):
         send_x(j).wait_recv()
         relay(j).start()
+
+        @pl.when(j < n_chunks - AHEAD)
+        def _():
+            bring(j + AHEAD)
+
         load_b(j).wait()
         send_d(j).wait_recv()
         relay(j).wait_recv()
@@ -177,7 +185,7 @@
     for j in range(n_chunks - LAG, n_chunks):
         send_c(j, 1).start()
 
-    @pl.loop(1, n_chunks)
+    @pl.loop(1, n_chunks - LAG)
     def _(j):
         finish(j)
 
@@ -198,6 +206,15 @@
         send_x(j).wait_send()
         send_d(j).wait_send()
         relay(j).wait_send()
+
+    @pl.loop(0, n_chunks - LAG)
+    def _(j):
+        for h in range(2):
+            send_c(j, h).wait_send()
+
+    for j in range(n_chunks - LAG, n_chunks):
+        finish(j)
+    for j in range(n_chunks - LAG, n_chunks):
         for h in range(2):
             send_c(j, h).wait_send()
 

time: 226 us -> 226 us (level)
  no operation moved by 1% of the time
where the time goes in v5:
time: 226 us
  Pallas kernels  224 us (99%)
    pallas_call x1, Pallas kernels, device_block(): pl.pallas_call(kernel, out_shape=pltpu.VMEM((rows, n), jnp.bfloat16), in_...  224 us

profile of v5, /device:TPU:1, one launch (start us, length us, event | category | flops | bytes accessed | tf_op | source)
XLA Modules:
  0.0 226.3 jit_solution(6991586458852742184)
XLA Ops:
  0.0 224.3 %shard_map.28 = bf16[384,5120]{1,0:T(8,128)(2,1)S(1)} custom-call(bf16[384,6144]{1,0:T(8,128)(2,1)} %a_ref.1, bf16[768,5120]{1,0:T(8,128)(2,1)} %b_ref.1), custom_call_target="tpu_custom_call" | custom-call | tf_op jit(solution)/shard_map/pallas_call | solution.py:231
  224.3 1.9 copy.4

commit v6 on v5

--- a/solution.py
+++ b/solution.py
@@ -81,9 +81,10 @@
             src_ref=b_buf.at[j, slot(2), :], dst_ref=b_buf.at[j, slot(3), :],
             send_sem=r_snd_sem.at[j], recv_sem=r_rcv_sem.at[j], device_id=to_d, device_id_type=MESH)
 
-    def send_c(j, h):
-        return pltpu.make_async_remote_copy(
-            src_ref=p_snd.at[j, pl.ds(h * half, half), :], dst_ref=p_rcv.at[j, pl.ds(h * half, half), :],
+    def send_c(j, start, size):
+        h = start // half
+        return pltpu.make_async_remote_copy(
+            src_ref=p_snd.at[j, pl.ds(start, size), :], dst_ref=p_rcv.at[j, pl.ds(start, size), :],
             send_sem=c_snd_sem.at[j, h], recv_sem=c_rcv_sem.at[j, h], device_id=to_y, device_id_type=MESH)
 
     load_first().start()
@@ -131,12 +132,14 @@
     for place in range(4):
         load_a(place).wait()
 
-    def part(j, h):
-        p_snd[j, pl.ds(h * half, half), :] = jnp.dot(
-            a_nbr[pl.ds(h * half, half), :], b_buf[j], preferred_element_type=jnp.float32)
-
-    @pl.loop(0, n_chunks)
-    def _(j):
+    def part(j, start, size):
+        p_snd[j, pl.ds(start, size), :] = jnp.dot(
+            a_nbr[pl.ds(start, size), :], b_buf[j], preferred_element_type=jnp.float32)
+
+    def own(j):
+        p_own[j] = jnp.dot(a_own[...], b_buf[j], preferred_element_type=jnp.float32)
+
+    def gather(j):
         send_x(j).wait_recv()
         relay(j).start()
 
@@ -148,46 +151,55 @@
         send_d(j).wait_recv()
         relay(j).wait_recv()
 
+    @pl.loop(0, LAG)
+    def _(j):
+        gather(j)
+
         @pl.when(j == 0)
         def _():
             for i in range(4):
                 send_a(i).wait_recv()
 
+        part(j, 0, half)
+        own(j)
+        send_c(j, 0, half).start()
+
+    @pl.loop(LAG, n_chunks)
+    def _(j):
+        gather(j)
+
         @pl.when(j == LAG)
         def _():
             for i in range(4, last + 1):
                 send_a(i).wait_recv()
 
-        part(j, 0)
-
-        @pl.when(j >= LAG)
-        def _():
-            part(j - LAG, 1)
-
-        p_own[j] = jnp.dot(a_own[...], b_buf[j], preferred_element_type=jnp.float32)
-        send_c(j, 0).start()
-
-        @pl.when(j >= LAG)
-        def _():
-            send_c(j - LAG, 1).start()
-
-    @pl.loop(n_chunks - LAG, n_chunks)
-    def _(j):
-        part(j, 1)
-
-    def finish(j):
-        for h in range(2):
-            send_c(j, h).wait_recv()
-            piece = pl.ds(h * half, half)
-            c_ref[piece, cols(j)] = (p_own[j, piece, :] + p_rcv[j, piece, :]).astype(c_ref.dtype)
-
-    finish(0)
-    for j in range(n_chunks - LAG, n_chunks):
-        send_c(j, 1).start()
-
-    @pl.loop(1, n_chunks - LAG)
-    def _(j):
-        finish(j)
+            @pl.loop(0, LAG)
+            def _(i):
+                part(i, half, half)
+
+        part(j, 0, rows)
+        own(j)
+
+        @pl.when(j == LAG)
+        def _():
+            for i in range(LAG):
+                send_c(i, half, half).start()
+
+        send_c(j, 0, rows).start()
+
+    def finish(j, start, size):
+        send_c(j, start, size).wait_recv()
+        piece = pl.ds(start, size)
+        c_ref[piece, cols(j)] = (p_own[j, piece, :] + p_rcv[j, piece, :]).astype(c_ref.dtype)
+
+    @pl.loop(0, LAG)
+    def _(j):
+        finish(j, 0, half)
+        finish(j, half, half)
+
+    @pl.loop(LAG, n_chunks - 2)
+    def _(j):
+        finish(j, 0, rows)
 
     for i in range(last):
         send_a(i).wait_send()
@@ -207,16 +219,19 @@
         send_d(j).wait_send()
         relay(j).wait_send()
 
-    @pl.loop(0, n_chunks - LAG)
-    def _(j):
-        for h in range(2):
-            send_c(j, h).wait_send()
-
-    for j in range(n_chunks - LAG, n_chunks):
-        finish(j)
-    for j in range(n_chunks - LAG, n_chunks):
-        for h in range(2):
-            send_c(j, h).wait_send()
+    @pl.loop(0, LAG)
+    def _(j):
+        send_c(j, 0, half).wait_send()
+        send_c(j, half, half).wait_send()
+
+    @pl.loop(LAG, n_chunks - 2)
+    def _(j):
+        send_c(j, 0, rows).wait_send()
+
+    for j in range(n_chunks - 2, n_chunks):
+        finish(j, 0, rows)
+    for j in range(n_chunks - 2, n_chunks):
+        send_c(j, 0, rows).wait_send()
 
 
 def solution(mesh):

time: 226 us -> 226 us (level)
  no operation moved by 1% of the time
where the time goes in v6:
time: 226 us
  Pallas kernels  224 us (99%)
    pallas_call x1, Pallas kernels, device_block(): pl.pallas_call(kernel, out_shape=pltpu.VMEM((rows, n), jnp.bfloat16), in_...  224 us

profile of v6, /device:TPU:1, one launch (start us, length us, event | category | flops | bytes accessed | tf_op | source)
XLA Modules:
  0.0 226.3 jit_solution(5362336317072295373)
XLA Ops:
  0.0 224.4 %shard_map.28 = bf16[384,5120]{1,0:T(8,128)(2,1)S(1)} custom-call(bf16[384,6144]{1,0:T(8,128)(2,1)} %a_ref.1, bf16[768,5120]{1,0:T(8,128)(2,1)} %b_ref.1), custom_call_target="tpu_custom_call" | custom-call | tf_op jit(solution)/shard_map/pallas_call | solution.py:246
  224.4 1.9 copy.4

commit v7 on v5

--- a/solution.py
+++ b/solution.py
@@ -9,6 +9,7 @@
 TN = 512
 LAG = 2
 AHEAD = 2
+PARTS = 8
 EXTRA = 96
 
 
@@ -219,6 +220,19 @@
             send_c(j, h).wait_send()
 
 
+def put_out(c_ref, out_ref, sem):
+    rows = c_ref.shape[0] // PARTS
+
+    def copy(i):
+        piece = pl.ds(i * rows, rows)
+        return pltpu.make_async_copy(c_ref.at[piece], out_ref.at[piece], sem.at[i])
+
+    for i in range(PARTS):
+        copy(i).start()
+    for i in range(PARTS):
+        copy(i).wait()
+
+
 def solution(mesh):
     all_axes = ("depth", "row", "col")
 
@@ -228,7 +242,7 @@
         k = 4 * k_rows
         n_chunks = n // TN
         dma = pltpu.SemaphoreType.DMA
-        return pl.pallas_call(
+        c = pl.pallas_call(
             kernel,
             out_shape=pltpu.VMEM((rows, n), jnp.bfloat16),
             in_specs=[pl.BlockSpec(memory_space=pl.ANY)] * 2,
@@ -254,6 +268,14 @@
             compiler_params=pltpu.CompilerParams(
                 collective_id=0, has_side_effects=True, vmem_limit_bytes=67043328 - 2 * rows * n),
         )(a_rows, b_rows)
+        return pl.pallas_call(
+            put_out,
+            out_shape=jax.ShapeDtypeStruct((rows, n), jnp.bfloat16),
+            in_specs=[pl.BlockSpec(memory_space=pltpu.VMEM)],
+            out_specs=pl.BlockSpec(memory_space=pl.ANY),
+            scratch_shapes=[dma((PARTS,))],
+            compiler_params=pltpu.CompilerParams(vmem_limit_bytes=2 ** 20),
+        )(pltpu.with_memory_space_constraint(c, pltpu.VMEM))
 
     return jax.shard_map(device_block, mesh=mesh, in_specs=(P(all_axes, None), P(all_axes, None)),
                          out_specs=P(all_axes, None), check_vma=False)

time: 226 us -> 226 us (level)
  no operation moved by 1% of the time
where the time goes in v7:
time: 226 us
  Pallas kernels  226 us (100%)
    pallas_call x1, Pallas kernels, device_block(): pl.pallas_call(kernel, out_shape=pltpu.VMEM((rows, n), jnp.bfloat16), in_...  224 us

profile of v7, /device:TPU:1, one launch (start us, length us, event | category | flops | bytes accessed | tf_op | source)
XLA Modules:
  0.0 226.3 jit_solution(14877831489951798678)
XLA Ops:
  0.0 224.3 %shard_map.28.c_ref = bf16[384,5120]{1,0:T(8,128)(2,1)S(1)} custom-call(bf16[384,6144]{1,0:T(8,128)(2,1)} %a_ref.1, bf16[768,5120]{1,0:T(8,128)(2,1)} %b_ref.1), custom_call_target="tpu_custom_call" | custom-call | tf_op jit(solution)/shard_map/pallas_call | solution.py:245
  224.3 2.0 shard_map.29

commit v8 on v5

--- a/solution.py
+++ b/solution.py
@@ -9,13 +9,14 @@
 TN = 512
 LAG = 2
 AHEAD = 2
+ROUND = 16
 EXTRA = 96
 
 
 def kernel(a_ref, b_ref, c_ref, b_buf, a_own, a_nbr, p_own, p_snd, p_rcv, a_first, a_fwd,
            ld_f, ld_a, ld_b, a_snd_sem, a_rcv_sem, x_snd_sem, x_rcv_sem, d_snd_sem, d_rcv_sem,
            r_snd_sem, r_rcv_sem, c_snd_sem, c_rcv_sem, f_snd_sem, f_rcv_sem, fwd_sem,
-           pair_sem, core_sem):
+           pair_sem, core_sem, round_buf, round_snd, round_rcv):
     depth, row, col = lax.axis_index("depth"), lax.axis_index("row"), lax.axis_index("col")
     to_y, to_x, to_d = {"col": 1 - col}, {"row": 1 - row}, {"depth": 1 - depth}
     rows, k_rows = a_ref.shape[0], b_ref.shape[0]
@@ -81,6 +82,23 @@
             src_ref=b_buf.at[j, slot(2), :], dst_ref=b_buf.at[j, slot(3), :],
             send_sem=r_snd_sem.at[j], recv_sem=r_rcv_sem.at[j], device_id=to_d, device_id_type=MESH)
 
+    tail_rows = pl.ds(rows - ROUND, ROUND)
+    source = (depth == 1) & (row == 0) & (col == 1)
+    first_relay = (depth == 1) & (row == 1) & (col == 1)
+    second_relay = (depth == 1) & (row == 1) & (col == 0)
+
+    def send_tail():
+        return pltpu.make_async_remote_copy(
+            src_ref=p_snd.at[n_chunks - 1, tail_rows, :], dst_ref=p_rcv.at[n_chunks - 1, tail_rows, :],
+            send_sem=round_snd.at[0], recv_sem=round_rcv.at[0], device_id=to_y, device_id_type=MESH)
+
+    def go_round(step):
+        src = p_snd.at[n_chunks - 1, tail_rows, :] if step == 0 else round_buf
+        dst = p_rcv.at[n_chunks - 1, tail_rows, :] if step == 2 else round_buf
+        return pltpu.make_async_remote_copy(
+            src_ref=src, dst_ref=dst, send_sem=round_snd.at[1], recv_sem=round_rcv.at[0 if step == 2 else 1],
+            device_id=to_y if step == 1 else to_x, device_id_type=MESH)
+
     def send_c(j, h):
         return pltpu.make_async_remote_copy(
             src_ref=p_snd.at[j, pl.ds(h * half, half), :], dst_ref=p_rcv.at[j, pl.ds(h * half, half), :],
@@ -175,15 +193,39 @@
     def _(j):
         part(j, 1)
 
+    def send_last():
+        piece = pl.ds(half, half - ROUND)
+        return pltpu.make_async_remote_copy(
+            src_ref=p_snd.at[n_chunks - 1, piece, :], dst_ref=p_rcv.at[n_chunks - 1, piece, :],
+            send_sem=c_snd_sem.at[n_chunks - 1, 1], recv_sem=c_rcv_sem.at[n_chunks - 1, 1],
+            device_id=to_y, device_id_type=MESH)
+
+    def add(j, piece):
+        c_ref[piece, cols(j)] = (p_own[j, piece, :] + p_rcv[j, piece, :]).astype(c_ref.dtype)
+
     def finish(j):
         for h in range(2):
             send_c(j, h).wait_recv()
-            piece = pl.ds(h * half, half)
-            c_ref[piece, cols(j)] = (p_own[j, piece, :] + p_rcv[j, piece, :]).astype(c_ref.dtype)
+            add(j, pl.ds(h * half, half))
 
     finish(0)
-    for j in range(n_chunks - LAG, n_chunks):
+    for j in range(n_chunks - LAG, n_chunks - 1):
         send_c(j, 1).start()
+
+    @pl.when(source)
+    def _():
+        go_round(0).start()
+
+    @pl.when(first_relay)
+    def _():
+        go_round(0).wait_recv()
+        go_round(1).start()
+
+    send_last().start()
+
+    @pl.when(jnp.logical_not(source))
+    def _():
+        send_tail().start()
 
     @pl.loop(1, n_chunks - LAG)
     def _(j):
@@ -212,11 +254,33 @@
         for h in range(2):
             send_c(j, h).wait_send()
 
-    for j in range(n_chunks - LAG, n_chunks):
+    for j in range(n_chunks - LAG, n_chunks - 1):
         finish(j)
-    for j in range(n_chunks - LAG, n_chunks):
         for h in range(2):
             send_c(j, h).wait_send()
+
+    @pl.when(second_relay)
+    def _():
+        go_round(1).wait_recv()
+        go_round(2).start()
+
+    send_c(n_chunks - 1, 0).wait_recv()
+    add(n_chunks - 1, pl.ds(0, half))
+    send_last().wait_recv()
+    add(n_chunks - 1, pl.ds(half, half - ROUND))
+    send_tail().wait_recv()
+    add(n_chunks - 1, tail_rows)
+
+    @pl.when(source | first_relay | second_relay)
+    def _():
+        go_round(0).wait_send()
+
+    send_c(n_chunks - 1, 0).wait_send()
+    send_last().wait_send()
+
+    @pl.when(jnp.logical_not(source))
+    def _():
+        send_tail().wait_send()
 
 
 def solution(mesh):
@@ -250,6 +314,7 @@
                 dma((n_chunks, 2)), dma((n_chunks, 2)),
                 dma, dma, dma,
                 pltpu.SemaphoreType.REGULAR, pltpu.SemaphoreType.REGULAR,
+                pltpu.VMEM((ROUND, TN), jnp.float32), dma((2,)), dma((2,)),
             ],
             compiler_params=pltpu.CompilerParams(
                 collective_id=0, has_side_effects=True, vmem_limit_bytes=67043328 - 2 * rows * n),

time: 226 us -> 226 us (level)
  no operation moved by 1% of the time
where the time goes in v8:
time: 226 us
  Pallas kernels  224 us (99%)
    pallas_call x1, Pallas kernels, device_block(): pl.pallas_call(kernel, out_shape=pltpu.VMEM((rows, n), jnp.bfloat16), in_...  224 us

profile of v8, /device:TPU:1, one launch (start us, length us, event | category | flops | bytes accessed | tf_op | source)
XLA Modules:
  0.0 226.0 jit_solution(1174830003653823576)
XLA Ops:
  0.0 224.0 %shard_map.28 = bf16[384,5120]{1,0:T(8,128)(2,1)S(1)} custom-call(bf16[384,6144]{1,0:T(8,128)(2,1)} %a_ref.1, bf16[768,5120]{1,0:T(8,128)(2,1)} %b_ref.1), custom_call_target="tpu_custom_call" | custom-call | tf_op jit(solution)/shard_map/pallas_call | solution.py:295
  224.0 1.9 copy.4

commit v9 on v8

--- a/solution.py
+++ b/solution.py
@@ -111,8 +111,11 @@
         pl.semaphore_signal(barrier, inc=1, device_id=peer, device_id_type=MESH)
     pl.semaphore_wait(barrier, 3 - 2 * depth)
 
+    for i in range(1, 4):
+        send_a(i).start()
     load_first().wait()
-    for i in range(last):
+    send_a(0).start()
+    for i in range(4, last):
         send_a(i).start()
 
     @pl.when(depth == 0)

time: 226 us -> 226 us (level)
  no operation moved by 1% of the time
where the time goes in v9:
time: 226 us; the launch traced here: 225 us
  Pallas kernels  223 us (99%)
    pallas_call x1, Pallas kernels, device_block(): pl.pallas_call(kernel, out_shape=pltpu.VMEM((rows, n), jnp.bfloat16), in_...  223 us

profile of v9, /device:TPU:1, one launch (start us, length us, event | category | flops | bytes accessed | tf_op | source)
XLA Modules:
  0.0 225.0 jit_solution(10963426013203174169)
XLA Ops:
  0.0 223.1 %shard_map.28 = bf16[384,5120]{1,0:T(8,128)(2,1)S(1)} custom-call(bf16[384,6144]{1,0:T(8,128)(2,1)} %a_ref.1, bf16[768,5120]{1,0:T(8,128)(2,1)} %b_ref.1), custom_call_target="tpu_custom_call" | custom-call | tf_op jit(solution)/shard_map/pallas_call | solution.py:298
  223.1 1.9 copy.4

commit v10 on v8

--- a/solution.py
+++ b/solution.py
@@ -13,8 +13,8 @@
 EXTRA = 96
 
 
-def kernel(a_ref, b_ref, c_ref, b_buf, a_own, a_nbr, p_own, p_snd, p_rcv, a_first, a_fwd,
-           ld_f, ld_a, ld_b, a_snd_sem, a_rcv_sem, x_snd_sem, x_rcv_sem, d_snd_sem, d_rcv_sem,
+def kernel(a_ref, b_ref, c_ref, b_buf, a_own, a_nbr, p_own, p_snd, p_rcv, a_fwd,
+           ld_a, ld_b, a_snd_sem, a_rcv_sem, x_snd_sem, x_rcv_sem, d_snd_sem, d_rcv_sem,
            r_snd_sem, r_rcv_sem, c_snd_sem, c_rcv_sem, f_snd_sem, f_rcv_sem, fwd_sem,
            pair_sem, core_sem, round_buf, round_snd, round_rcv):
     depth, row, col = lax.axis_index("depth"), lax.axis_index("row"), lax.axis_index("col")
@@ -40,9 +40,6 @@
     def load_b(j):
         return pltpu.make_async_copy(b_ref.at[:, cols(j)], b_buf.at[j, slot(0), :], ld_b.at[j])
 
-    def load_first():
-        return pltpu.make_async_copy(a_ref.at[pl.ds(0, half), k_block(0, 1 - col)], a_first, ld_f)
-
     pieces = [(0, half, p) for p in range(4)] + [(half, half, p) for p in range(3)]
     pieces += [(half, half - EXTRA, 3), (rows - EXTRA, EXTRA, 3)]
     last = len(pieces) - 1
@@ -50,7 +47,7 @@
     def send_a(i):
         start, size, place = pieces[i]
         return pltpu.make_async_remote_copy(
-            src_ref=a_first if i == 0 else a_ref.at[pl.ds(start, size), k_block(place, 1 - col)],
+            src_ref=a_ref.at[pl.ds(start, size), k_block(place, 1 - col)],
             dst_ref=a_nbr.at[pl.ds(start, size), slot(place)],
             send_sem=a_snd_sem.at[i], recv_sem=a_rcv_sem.at[i], device_id=to_y, device_id_type=MESH)
 
@@ -104,14 +101,11 @@
             src_ref=p_snd.at[j, pl.ds(h * half, half), :], dst_ref=p_rcv.at[j, pl.ds(h * half, half), :],
             send_sem=c_snd_sem.at[j, h], recv_sem=c_rcv_sem.at[j, h], device_id=to_y, device_id_type=MESH)
 
-    load_first().start()
-
     barrier = pltpu.get_barrier_semaphore()
     for peer in (to_y, {"depth": 0, "row": lax.rem(row + 1 - depth, 2)}):
         pl.semaphore_signal(barrier, inc=1, device_id=peer, device_id_type=MESH)
     pl.semaphore_wait(barrier, 3 - 2 * depth)
 
-    load_first().wait()
     for i in range(last):
         send_a(i).start()
 
@@ -304,9 +298,8 @@
                 pltpu.VMEM((n_chunks, rows, TN), jnp.float32),
                 pltpu.VMEM((n_chunks, rows, TN), jnp.float32),
                 pltpu.VMEM((n_chunks, rows, TN), jnp.float32),
-                pltpu.VMEM((rows // 2, k_rows), jnp.bfloat16),
                 pltpu.VMEM((EXTRA, k_rows), jnp.bfloat16),
-                dma, dma((4,)), dma((n_chunks,)),
+                dma((4,)), dma((n_chunks,)),
                 dma((9,)), dma((9,)),
                 dma((n_chunks,)), dma((n_chunks,)),
                 dma((n_chunks,)), dma((n_chunks,)),

time: 226 us -> 226 us (level)
  no operation moved by 1% of the time
where the time goes in v10:
time: 226 us; the launch traced here: 225 us
  Pallas kernels  223 us (99%)
    pallas_call x1, Pallas kernels, device_block(): pl.pallas_call(kernel, out_shape=pltpu.VMEM((rows, n), jnp.bfloat16), in_...  223 us

profile of v10, /device:TPU:1, one launch (start us, length us, event | category | flops | bytes accessed | tf_op | source)
XLA Modules:
  0.0 225.0 jit_solution(14666880606690416590)
XLA Ops:
  0.0 223.1 %shard_map.28 = bf16[384,5120]{1,0:T(8,128)(2,1)S(1)} custom-call(bf16[384,6144]{1,0:T(8,128)(2,1)} %a_ref.1, bf16[768,5120]{1,0:T(8,128)(2,1)} %b_ref.1), custom_call_target="tpu_custom_call" | custom-call | tf_op jit(solution)/shard_map/pallas_call | solution.py:289
  223.1 1.9 copy.4

commit v11 on v10

--- a/solution.py
+++ b/solution.py
@@ -10,7 +10,7 @@
 LAG = 2
 AHEAD = 2
 ROUND = 16
-EXTRA = 96
+EXTRA = 112
 
 
 def kernel(a_ref, b_ref, c_ref, b_buf, a_own, a_nbr, p_own, p_snd, p_rcv, a_fwd,

time: 226 us -> 225 us (level)
  no operation moved by 1% of the time
where the time goes in v11:
time: 225 us
  Pallas kernels  223 us (99%)
    pallas_call x1, Pallas kernels, device_block(): pl.pallas_call(kernel, out_shape=pltpu.VMEM((rows, n), jnp.bfloat16), in_...  223 us

profile of v11, /device:TPU:1, one launch (start us, length us, event | category | flops | bytes accessed | tf_op | source)
XLA Modules:
  0.0 225.0 jit_solution(8516215247305410837)
XLA Ops:
  0.0 223.1 %shard_map.28 = bf16[384,5120]{1,0:T(8,128)(2,1)S(1)} custom-call(bf16[384,6144]{1,0:T(8,128)(2,1)} %a_ref.1, bf16[768,5120]{1,0:T(8,128)(2,1)} %b_ref.1), custom_call_target="tpu_custom_call" | custom-call | tf_op jit(solution)/shard_map/pallas_call | solution.py:289
  223.1 1.9 copy.4

commit v12 on v11

--- a/solution.py
+++ b/solution.py
@@ -13,7 +13,7 @@
 EXTRA = 112
 
 
-def kernel(a_ref, b_ref, c_ref, b_buf, a_own, a_nbr, p_own, p_snd, p_rcv, a_fwd,
+def kernel(a_ref, b_ref, c_ref, own_ref, nbr_ref, b_buf, a_own, a_nbr, p_own, p_snd, p_rcv, a_fwd,
            ld_a, ld_b, a_snd_sem, a_rcv_sem, x_snd_sem, x_rcv_sem, d_snd_sem, d_rcv_sem,
            r_snd_sem, r_rcv_sem, c_snd_sem, c_rcv_sem, f_snd_sem, f_rcv_sem, fwd_sem,
            pair_sem, core_sem, round_buf, round_snd, round_rcv):
@@ -21,7 +21,7 @@
     to_y, to_x, to_d = {"col": 1 - col}, {"row": 1 - row}, {"depth": 1 - depth}
     rows, k_rows = a_ref.shape[0], b_ref.shape[0]
     half = rows // 2
-    n_chunks = b_buf.shape[0]
+    n_chunks, n_here = b_buf.shape[0], p_own.shape[0]
 
     def k_block(place, c):
         d = 1 - depth if place % 2 else depth
@@ -40,9 +40,9 @@
     def load_b(j):
         return pltpu.make_async_copy(b_ref.at[:, cols(j)], b_buf.at[j, slot(0), :], ld_b.at[j])
 
-    pieces = [(0, half, p) for p in range(4)] + [(half, half, p) for p in range(3)]
-    pieces += [(half, half - EXTRA, 3), (rows - EXTRA, EXTRA, 3)]
-    last = len(pieces) - 1
+    pieces = [(0, half, p) for p in range(4)] + [(half, half, p) for p in range(2)]
+    pieces += [(half, half - EXTRA, p) for p in (2, 3)] + [(rows - EXTRA, EXTRA, p) for p in (2, 3)]
+    last = len(pieces) - 2
 
     def send_a(i):
         start, size, place = pieces[i]
@@ -51,17 +51,17 @@
             dst_ref=a_nbr.at[pl.ds(start, size), slot(place)],
             send_sem=a_snd_sem.at[i], recv_sem=a_rcv_sem.at[i], device_id=to_y, device_id_type=MESH)
 
-    def hand_over():
-        start, size, place = pieces[last]
-        return pltpu.make_async_remote_copy(
-            src_ref=a_ref.at[pl.ds(start, size), k_block(place, 1 - col)], dst_ref=a_fwd,
-            send_sem=f_snd_sem, recv_sem=f_rcv_sem, device_id=to_d, device_id_type=MESH)
-
-    def send_for_other():
-        start, size, place = pieces[last]
-        return pltpu.make_async_remote_copy(
-            src_ref=a_fwd, dst_ref=a_nbr.at[pl.ds(start, size), slot(place)],
-            send_sem=fwd_sem, recv_sem=a_rcv_sem.at[last],
+    def hand_over(i):
+        start, size, place = pieces[last + i]
+        return pltpu.make_async_remote_copy(
+            src_ref=a_ref.at[pl.ds(start, size), k_block(place, 1 - col)], dst_ref=a_fwd.at[i],
+            send_sem=f_snd_sem.at[i], recv_sem=f_rcv_sem.at[i], device_id=to_d, device_id_type=MESH)
+
+    def send_for_other(i):
+        start, size, place = pieces[last + i]
+        return pltpu.make_async_remote_copy(
+            src_ref=a_fwd.at[i], dst_ref=a_nbr.at[pl.ds(start, size), slot(place)],
+            send_sem=fwd_sem.at[i], recv_sem=a_rcv_sem.at[last + i],
             device_id={"col": 1 - col, "depth": 0}, device_id_type=MESH)
 
     def send_x(j):
@@ -86,12 +86,12 @@
 
     def send_tail():
         return pltpu.make_async_remote_copy(
-            src_ref=p_snd.at[n_chunks - 1, tail_rows, :], dst_ref=p_rcv.at[n_chunks - 1, tail_rows, :],
+            src_ref=p_snd.at[n_here - 1, tail_rows, :], dst_ref=p_rcv.at[n_here - 1, tail_rows, :],
             send_sem=round_snd.at[0], recv_sem=round_rcv.at[0], device_id=to_y, device_id_type=MESH)
 
     def go_round(step):
-        src = p_snd.at[n_chunks - 1, tail_rows, :] if step == 0 else round_buf
-        dst = p_rcv.at[n_chunks - 1, tail_rows, :] if step == 2 else round_buf
+        src = p_snd.at[n_here - 1, tail_rows, :] if step == 0 else round_buf
+        dst = p_rcv.at[n_here - 1, tail_rows, :] if step == 2 else round_buf
         return pltpu.make_async_remote_copy(
             src_ref=src, dst_ref=dst, send_sem=round_snd.at[1], recv_sem=round_rcv.at[0 if step == 2 else 1],
             device_id=to_y if step == 1 else to_x, device_id_type=MESH)
@@ -111,14 +111,16 @@
 
     @pl.when(depth == 0)
     def _():
-        hand_over().start()
+        for i in range(2):
+            hand_over(i).start()
         pl.semaphore_signal(pair_sem, inc=1, device_id=to_x, device_id_type=MESH)
         pl.semaphore_wait(pair_sem, 1)
         pl.semaphore_signal(core_sem, inc=1, device_id=to_d, device_id_type=MESH)
 
     @pl.when(depth == 1)
     def _():
-        send_a(last).start()
+        for i in range(2):
+            send_a(last + i).start()
         pl.semaphore_wait(core_sem, 1)
 
     @pl.loop(0, n_chunks)
@@ -137,8 +139,9 @@
 
     @pl.when(depth == 1)
     def _():
-        hand_over().wait_recv()
-        send_for_other().start()
+        for i in range(2):
+            hand_over(i).wait_recv()
+            send_for_other(i).start()
 
     for place in range(4):
         load_a(place).wait()
@@ -147,8 +150,7 @@
         p_snd[j, pl.ds(h * half, half), :] = jnp.dot(
             a_nbr[pl.ds(h * half, half), :], b_buf[j], preferred_element_type=jnp.float32)
 
-    @pl.loop(0, n_chunks)
-    def _(j):
+    def gather(j):
         send_x(j).wait_recv()
         relay(j).start()
 
@@ -160,6 +162,10 @@
         send_d(j).wait_recv()
         relay(j).wait_recv()
 
+    @pl.loop(0, n_here)
+    def _(j):
+        gather(j)
+
         @pl.when(j == 0)
         def _():
             for i in range(4):
@@ -167,7 +173,7 @@
 
         @pl.when(j == LAG)
         def _():
-            for i in range(4, last + 1):
+            for i in range(4, last + 2):
                 send_a(i).wait_recv()
 
         part(j, 0)
@@ -183,15 +189,15 @@
         def _():
             send_c(j - LAG, 1).start()
 
-    @pl.loop(n_chunks - LAG, n_chunks)
+    @pl.loop(n_here - LAG, n_here)
     def _(j):
         part(j, 1)
 
     def send_last():
         piece = pl.ds(half, half - ROUND)
         return pltpu.make_async_remote_copy(
-            src_ref=p_snd.at[n_chunks - 1, piece, :], dst_ref=p_rcv.at[n_chunks - 1, piece, :],
-            send_sem=c_snd_sem.at[n_chunks - 1, 1], recv_sem=c_rcv_sem.at[n_chunks - 1, 1],
+            src_ref=p_snd.at[n_here - 1, piece, :], dst_ref=p_rcv.at[n_here - 1, piece, :],
+            send_sem=c_snd_sem.at[n_here - 1, 1], recv_sem=c_rcv_sem.at[n_here - 1, 1],
             device_id=to_y, device_id_type=MESH)
 
     def add(j, piece):
@@ -203,7 +209,7 @@
             add(j, pl.ds(h * half, half))
 
     finish(0)
-    for j in range(n_chunks - LAG, n_chunks - 1):
+    for j in range(n_here - LAG, n_here - 1):
         send_c(j, 1).start()
 
     @pl.when(source)
@@ -221,7 +227,11 @@
     def _():
         send_tail().start()
 
-    @pl.loop(1, n_chunks - LAG)
+    gather(n_chunks - 1)
+    nbr_ref[...] = jnp.dot(a_nbr[...], b_buf[n_chunks - 1], preferred_element_type=jnp.float32)
+    own_ref[...] = jnp.dot(a_own[...], b_buf[n_chunks - 1], preferred_element_type=jnp.float32)
+
+    @pl.loop(1, n_here - LAG)
     def _(j):
         finish(j)
 
@@ -230,12 +240,14 @@
 
     @pl.when(depth == 0)
     def _():
-        hand_over().wait_send()
+        for i in range(2):
+            hand_over(i).wait_send()
 
     @pl.when(depth == 1)
     def _():
-        send_a(last).wait_send()
-        send_for_other().wait_send()
+        for i in range(2):
+            send_a(last + i).wait_send()
+            send_for_other(i).wait_send()
 
     @pl.loop(0, n_chunks)
     def _(j):
@@ -243,12 +255,12 @@
         send_d(j).wait_send()
         relay(j).wait_send()
 
-    @pl.loop(0, n_chunks - LAG)
+    @pl.loop(0, n_here - LAG)
     def _(j):
         for h in range(2):
             send_c(j, h).wait_send()
 
-    for j in range(n_chunks - LAG, n_chunks - 1):
+    for j in range(n_here - LAG, n_here - 1):
         finish(j)
         for h in range(2):
             send_c(j, h).wait_send()
@@ -258,23 +270,59 @@
         go_round(1).wait_recv()
         go_round(2).start()
 
-    send_c(n_chunks - 1, 0).wait_recv()
-    add(n_chunks - 1, pl.ds(0, half))
+    send_c(n_here - 1, 0).wait_recv()
+    add(n_here - 1, pl.ds(0, half))
     send_last().wait_recv()
-    add(n_chunks - 1, pl.ds(half, half - ROUND))
+    add(n_here - 1, pl.ds(half, half - ROUND))
     send_tail().wait_recv()
-    add(n_chunks - 1, tail_rows)
+    add(n_here - 1, tail_rows)
 
     @pl.when(source | first_relay | second_relay)
     def _():
         go_round(0).wait_send()
 
-    send_c(n_chunks - 1, 0).wait_send()
+    send_c(n_here - 1, 0).wait_send()
     send_last().wait_send()
 
     @pl.when(jnp.logical_not(source))
     def _():
         send_tail().wait_send()
+
+
+def last_kernel(own_ref, nbr_ref, out_ref, c_ref, rcv, snd_sem, rcv_sem):
+    to_y = {"col": 1 - lax.axis_index("col")}
+    half = own_ref.shape[0] // 2
+
+    def send(h):
+        piece = pl.ds(h * half, half)
+        return pltpu.make_async_remote_copy(
+            src_ref=nbr_ref.at[piece], dst_ref=rcv.at[piece], send_sem=snd_sem.at[h], recv_sem=rcv_sem.at[h],
+            device_id=to_y, device_id_type=MESH)
+
+    barrier = pltpu.get_barrier_semaphore()
+    pl.semaphore_signal(barrier, inc=1, device_id=to_y, device_id_type=MESH)
+    pl.semaphore_wait(barrier, 1)
+    for h in range(2):
+        send(h).start()
+    for h in range(2):
+        piece = pl.ds(h * half, half)
+        send(h).wait_recv()
+        c_ref[piece, :] = (own_ref[piece, :] + rcv[piece, :]).astype(c_ref.dtype)
+    for h in range(2):
+        send(h).wait_send()
+
+
+def write_first(c_ref, out_ref, sem):
+    copy = pltpu.make_async_copy(c_ref, out_ref.at[:, pl.ds(0, c_ref.shape[1])], sem)
+    copy.start()
+    copy.wait()
+
+
+def write_last(whole_ref, c_ref, out_ref, sem):
+    start = out_ref.shape[1] - c_ref.shape[1]
+    copy = pltpu.make_async_copy(c_ref, out_ref.at[:, pl.ds(start, c_ref.shape[1])], sem)
+    copy.start()
+    copy.wait()
 
 
 def solution(mesh):
@@ -286,32 +334,56 @@
         k = 4 * k_rows
         n_chunks = n // TN
         dma = pltpu.SemaphoreType.DMA
-        return pl.pallas_call(
+        n_here = n_chunks - 1
+        f32 = jnp.float32
+        vmem, any_space = pl.BlockSpec(memory_space=pltpu.VMEM), pl.BlockSpec(memory_space=pl.ANY)
+        kept = 2 * rows * n_here * TN + 8 * rows * TN
+        regular = pltpu.SemaphoreType.REGULAR
+        c, own, nbr = pl.pallas_call(
             kernel,
-            out_shape=pltpu.VMEM((rows, n), jnp.bfloat16),
-            in_specs=[pl.BlockSpec(memory_space=pl.ANY)] * 2,
-            out_specs=pl.BlockSpec(memory_space=pltpu.VMEM),
+            out_shape=(pltpu.VMEM((rows, n_here * TN), jnp.bfloat16),
+                       pltpu.VMEM((rows, TN), f32), pltpu.VMEM((rows, TN), f32)),
+            in_specs=[any_space] * 2,
+            out_specs=(vmem,) * 3,
             scratch_shapes=[
                 pltpu.VMEM((n_chunks, k, TN), jnp.bfloat16),
                 pltpu.VMEM((rows, k), jnp.bfloat16),
                 pltpu.VMEM((rows, k), jnp.bfloat16),
-                pltpu.VMEM((n_chunks, rows, TN), jnp.float32),
-                pltpu.VMEM((n_chunks, rows, TN), jnp.float32),
-                pltpu.VMEM((n_chunks, rows, TN), jnp.float32),
-                pltpu.VMEM((EXTRA, k_rows), jnp.bfloat16),
+                pltpu.VMEM((n_here, rows, TN), f32),
+                pltpu.VMEM((n_here, rows, TN), f32),
+                pltpu.VMEM((n_here, rows, TN), f32),
+                pltpu.VMEM((2, EXTRA, k_rows), jnp.bfloat16),
                 dma((4,)), dma((n_chunks,)),
-                dma((9,)), dma((9,)),
+                dma((10,)), dma((10,)),
                 dma((n_chunks,)), dma((n_chunks,)),
                 dma((n_chunks,)), dma((n_chunks,)),
                 dma((n_chunks,)), dma((n_chunks,)),
-                dma((n_chunks, 2)), dma((n_chunks, 2)),
-                dma, dma, dma,
-                pltpu.SemaphoreType.REGULAR, pltpu.SemaphoreType.REGULAR,
-                pltpu.VMEM((ROUND, TN), jnp.float32), dma((2,)), dma((2,)),
+                dma((n_here, 2)), dma((n_here, 2)),
+                dma((2,)), dma((2,)), dma((2,)),
+                regular, regular,
+                pltpu.VMEM((ROUND, TN), f32), dma((2,)), dma((2,)),
             ],
             compiler_params=pltpu.CompilerParams(
-                collective_id=0, has_side_effects=True, vmem_limit_bytes=67043328 - 2 * rows * n),
+                collective_id=0, has_side_effects=True, vmem_limit_bytes=67043328 - kept),
         )(a_rows, b_rows)
+        in_vmem = lambda x: pltpu.with_memory_space_constraint(x, pltpu.VMEM)
+        small = pltpu.CompilerParams(vmem_limit_bytes=2 ** 20)
+        whole = jax.ShapeDtypeStruct((rows, n), jnp.bfloat16)
+        out = pl.pallas_call(
+            write_first, out_shape=whole, in_specs=[vmem], out_specs=any_space,
+            scratch_shapes=[dma], compiler_params=small)(in_vmem(c))
+        c_last = pl.pallas_call(
+            last_kernel,
+            out_shape=pltpu.VMEM((rows, TN), jnp.bfloat16),
+            in_specs=[vmem, vmem, pl.BlockSpec(memory_space=pltpu.HBM)],
+            out_specs=vmem,
+            scratch_shapes=[pltpu.VMEM((rows, TN), f32), dma((2,)), dma((2,))],
+            compiler_params=pltpu.CompilerParams(
+                collective_id=1, has_side_effects=True, vmem_limit_bytes=2 ** 23),
+        )(in_vmem(own), in_vmem(nbr), pltpu.with_memory_space_constraint(out, pltpu.HBM))
+        return pl.pallas_call(
+            write_last, out_shape=whole, in_specs=[any_space, vmem], out_specs=any_space,
+            scratch_shapes=[dma], input_output_aliases={0: 0}, compiler_params=small)(out, in_vmem(c_last))
 
     return jax.shard_map(device_block, mesh=mesh, in_specs=(P(all_axes, None), P(all_axes, None)),
                          out_specs=P(all_axes, None), check_vma=False)

time: 225 us -> 225 us (level)
    pallas_call x1 -> x4, Pallas kernels: 223 us -> 225 us  [the longest x1 206 us: device_block(): pl.pallas_call(kernel, out_shape=(pltpu.VMEM((rows, n_here * TN), jnp.bfl...]
where the time goes in v12:
time: 225 us
  Pallas kernels  225 us (100%)
    pallas_call x1, Pallas kernels, device_block(): pl.pallas_call(kernel, out_shape=(pltpu.VMEM((rows, n_here * TN), jnp.bfl...  206 us
    pallas_call x1, Pallas kernels, device_block(): pl.pallas_call(last_kernel, out_shape=pltpu.VMEM((rows, TN), jnp.bfloat16...  16.4 us

profile of v12, /device:TPU:1, one launch (start us, length us, event | category | flops | bytes accessed | tf_op | source)
XLA Modules:
  0.0 225.2 jit_solution(13865514516579821481)
XLA Ops:
  0.0 206.2 %shard_map.28 = (bf16[384,4608]{1,0:T(8,128)(2,1)S(1)}, f32[384,512]{1,0:T(8,128)S(1)}, f32[384,512]{1,0:T(8,128)S(1)}) custom-call(bf16[384,6144]{1,0:T(8,128)(2,1)} %a_ref.1, bf16[768,5120]{1,0:T(8,128)(2,1)} %b_ref.1), custom_call_target="tpu_custom_call" | custom-call | tf_op jit(solution)/shard_map/pallas_call | solution.py:342
  206.2 1.8 shard_map.29.out_ref.whole_ref
  208.0 16.4 %shard_map.30.c_ref = bf16[384,512]{1,0:T(8,128)(2,1)S(1)} custom-call(f32[384,512]{1,0:T(8,128)S(1)} %get-tuple-element.9.own_ref, f32[384,512]{1,0:T(8,128)S(1)} %get-tuple-element.10.nbr_ref, bf16[384,5120]{1,0:T(8,128)(2,1)} %shard_map.29.out_ref.whole_ref), custom_call_target="tpu_custom_call" | custom-call | tf_op jit(solution)/shard_map/pallas_call | solution.py:375
  224.4 0.8 shard_map.31
